TPU v7x, 128 devices: a whole 4x4x4 slice. The times are simulated.
128 devices in a mesh: rows: 16 (over z_hi, x, core), cols: 8 (over y, z_lo).
Axes of the slice: x: 4, y: 4, z: 4 (z_hi: 2, z_lo: 2; z = z_hi * 2 + z_lo), core: 2. Of those that a mesh axis runs over, the one named last changes fastest.
Arguments:
- block_values: bfloat16 [65536, 128], P(('rows', 'cols')), may hold values from -6 to 6
- block_length: int32 [65536], P(('rows', 'cols')), may hold values from 1 to 128
- block_owner: int32 [65536], P(('rows', 'cols')), may hold values from 0 to 16383, as said below
- block_second: int32 [65536], P(('rows', 'cols')), may hold values from 0 to 16383, as said below
- block_third: int32 [65536, 128], P(('rows', 'cols')), may hold values from 0 to 32767
- live_blocks: int32 [128], P(('rows', 'cols')), may hold values from 1 to 512, as said below
- second_factor: bfloat16 [16384, 256], P('cols', 'rows')
- third_factor: bfloat16 [32768, 256], P('cols', 'rows'), may hold values from -6 to 6
Outputs:
- first_factor: float32 [16384, 256], P('cols', 'rows')
Inputs may be any that keep to these rules, and one draw needn't show every extreme that they name: `block_owner`: slot b lies on device d = b // 512 with index r along rows; its row lies in r * 16384 // 16 up to (r + 1) * 16384 // 16 - 1, the device's mode-1 slab. `block_second`: slot b lies on device d = b // 512 with index c along cols; its row lies in c * 16384 // 8 up to (c + 1) * 16384 // 8 - 1. `live_blocks`: some device uses all 512 slots in every draw.
All inputs are finite; a program needn't handle non-finite values.
Results may differ from a plain program's by a relative error of at most 0.0003.
Values may be sent and summed in bfloat16 or wider, within the bound.
No kernel may reach another device: no remote copies, remote signals or barrier semaphores. Data moves between devices by JAX's collectives and lax.ppermute only.
A program may use at most 128 MiB of HBM per device.

v0:
```python
import jax
import jax.numpy as jnp
from jax import lax
from jax.sharding import PartitionSpec as P

I_DEV = 128


def joined_along(blocks, dim):
    shape = list(blocks.shape[1:])
    shape[dim] *= blocks.shape[0]
    return jnp.moveaxis(blocks, 0, dim).reshape(shape)


def from_everyone(value, axis):
    size = lax.axis_size(axis)
    return lax.all_to_all(
        jnp.broadcast_to(value[None], (size, *value.shape)), axis, 0, 0, tiled=True
    )


def collect(value, axis, dim):
    return joined_along(from_everyone(value, axis), dim)


def gram_product(left, right):
    contract = (((0,), (0,)), ((), ()))
    return lax.dot_general(left, right, contract, preferred_element_type=jnp.float32)


def block_fold(values, third, table):
    group = values.shape[0]
    width = values.shape[1]
    picked = table[third.reshape(group * width)]
    scaled = values.reshape(group * width, 1).astype(jnp.float32) * picked.astype(jnp.float32)
    return jnp.sum(scaled.reshape(group, width, picked.shape[1]), axis=1)


def per_device(
    block_values,
    block_length,
    block_owner,
    block_second,
    block_third,
    live_blocks,
    second_factor,
    third_factor,
):
    n_rows = lax.axis_size("rows")
    n_cols = lax.axis_size("cols")
    row_at = lax.axis_index("rows")
    col_at = lax.axis_index("cols")
    contract = (((0,), (0,)), ((), ()))
    width = block_values.shape[1]
    lane = jnp.arange(width, dtype=jnp.int32)
    slab = I_DEV * n_cols
    owned = jnp.arange(slab, dtype=jnp.int32)
    second_range = lax.all_gather(second_factor, "rows", axis=1, tiled=True)
    third_part = collect(third_factor, "cols", 0)
    third_whole = lax.all_gather(third_part, "rows", axis=1, tiled=True)
    range_rows = second_range.shape[0]
    local_gram = gram_product(second_range, second_range)
    gram_second = lax.psum(local_gram, "cols") / (range_rows * n_cols)
    gram_third = gram_product(third_whole, third_whole) / third_whole.shape[0]
    gram = gram_second * gram_third
    nblk = block_values.shape[0]
    group = min(nblk, 128)
    count = live_blocks[0]

    def accumulate(step, total):
        start = step * group
        values = lax.dynamic_slice_in_dim(block_values, start, group, 0)
        lengths = lax.dynamic_slice_in_dim(block_length, start, group, 0)
        third = lax.dynamic_slice_in_dim(block_third, start, group, 0)
        second = lax.dynamic_slice_in_dim(block_second, start, group, 0)
        owner = lax.dynamic_slice_in_dim(block_owner, start, group, 0)
        slot = start + jnp.arange(group, dtype=jnp.int32)
        live = (lane[None, :] < lengths[:, None]) & (slot < count)[:, None]
        values = jnp.where(live, values, jnp.zeros((), jnp.bfloat16))
        fold = block_fold(values, third, third_whole)
        contrib = second_range[second - col_at * range_rows].astype(jnp.float32) * fold
        onehot = ((owner - row_at * slab)[:, None] == owned[None, :]).astype(jnp.float32)
        return total + lax.dot_general(
            onehot,
            contrib,
            contract,
            precision=lax.Precision.HIGHEST,
            preferred_element_type=jnp.float32,
        )

    start_total = jnp.zeros((slab, gram.shape[0]), jnp.float32)
    partial_rows = lax.fori_loop(0, nblk // group, accumulate, start_total)
    mine = lax.psum_scatter(partial_rows, "cols", scatter_dimension=0, tiled=True)
    factor = jnp.linalg.cholesky(gram)
    solved = jax.scipy.linalg.cho_solve((factor, True), mine.T).T
    moved = lax.all_to_all(
        lax.all_to_all(solved, "rows", split_axis=1, concat_axis=0, tiled=True),
        "cols",
        split_axis=0,
        concat_axis=0,
        tiled=True,
    )
    share = n_rows // n_cols
    owned_rows = mine.shape[0]
    reordered = moved.reshape(n_cols, share, owned_rows, moved.shape[1]).transpose(1, 0, 2, 3)
    return reordered.reshape(n_rows * owned_rows, moved.shape[1])


def solution(mesh):
    return jax.shard_map(
        per_device,
        mesh=mesh,
        in_specs=(
            P(("rows", "cols"), None),
            P(("rows", "cols")),
            P(("rows", "cols")),
            P(("rows", "cols")),
            P(("rows", "cols"), None),
            P(("rows", "cols")),
            P("cols", "rows"),
            P("cols", "rows"),
        ),
        out_specs=P("cols", "rows"),
        check_vma=False,
    )
```

profile of v0, /device:TPU:0, one launch (start us, length us, event | category | flops | bytes accessed | tf_op | source)
XLA Modules:
  0.0 622.8 jit_solution(15795296984549790997)
XLA Ops:
  7.3 1.0 broadcast_in_dim.48
  8.3 21.1 %all_to_all.30 = bf16[8,4096,16]{1,2,0:T(8,128)(2,1)S(1)} all-to-all(bf16[8,4096,16]{1,2,0:T(8,128)(2,1)S(1)} %broadcast_in_dim.48), channel_id=1, replica_groups=mesh['rows'=16,'cols'=8] {'cols'}, dimensions={0} | all-to-all | bytes 2097152 | tf_op jit(solution)/shard_map/all_to_all | solution.py:17
  29.4 1.1 copy.51
  30.6 28.7 %all-gather.3.cloned.1.call-done = bf16[2048,256]{0,1:T(8,128)(2,1)} async-done(((bf16[2048,16]{0,1:T(8,128)(2,1)}), bf16[2048,256]{0,1:T(8,128)(2,1)}) %all-gather.3.cloned.1.call-update) | async-done | bytes 1048592 | tf_op jit(solution)/shard_map/all_gather | solution.py:58
  59.3 2.8 fusion.24
  62.1 1.5 copy.43
  63.6 106.5 %all-gather.5.cloned.1.call-done = bf16[32768,256]{0,1:T(8,128)(2,1)} async-done(((bf16[32768,16]{0,1:T(8,128)(2,1)}), bf16[32768,256]{0,1:T(8,128)(2,1)}) %all-gather.5.cloned.1.call-update) | async-done | bytes 16777232 | tf_op jit(solution)/shard_map/all_gather | solution.py:60
  170.2 22.4 %copy.44 = bf16[32768,256]{1,0:T(8,128)(2,1)} copy(bf16[32768,256]{0,1:T(8,128)(2,1)} %all-gather.5.cloned.1.call-done) | data formatting | bytes 33554432
  192.6 321.0 %while.18 = (s32[]{:T(128)}, f32[1024,256]{1,0:T(8,128)S(1)}, s32[512]{0:T(512)}, s32[]{:T(128)}, s32[512]{0:T(512)}, /*index=5*/s32[]{:T(128)}, bf16[2048,256]{...) while((s32[]{:T(128)}, f32[1024,256]{1,0:T(8,128)S(1)}, ...), condition=%wide.region_7.8_spmd.clone, body=%wide.region_5.7_spmd.clone.sunk | while | flops 416057216 | bytes 28354028 | solution.py:92
  194.0 0.9 fusion.42
  194.8 0.9 constant_dynamic-slice_fusion.5
  195.8 68.7 %gather_fusion = bf16[16384,256]{1,0:T(8,128)(2,1)} fusion(bf16[32768,256]{1,0:T(8,128)(2,1)} %get-tuple-element.593, s32[16384]{0:T(1024)S(1)} %broadcast_clamp_fusion.2), kind=kCustom, calls=%fused_computation.1.clone.clone.1 | custom fusion | bytes 16842752 | tf_op jit(solution)/shard_map/while/body/eval_jaxpr/gather | solution.py:34
  264.5 5.5 fusion.43
  269.9 0.8 compare_select_fusion.4
  270.7 0.8 gather_fusion.1
  271.6 1.2 convolution_add_fusion.2
  274.2 0.9 fusion.42
  275.1 0.9 constant_dynamic-slice_fusion.5
  276.0 68.7 %gather_fusion = bf16[16384,256]{1,0:T(8,128)(2,1)} fusion(bf16[32768,256]{1,0:T(8,128)(2,1)} %get-tuple-element.593, s32[16384]{0:T(1024)S(1)} %broadcast_clamp_fusion.2), kind=kCustom, calls=%fused_computation.1.clone.clone.1 | custom fusion | bytes 16842752 | tf_op jit(solution)/shard_map/while/body/eval_jaxpr/gather | solution.py:34
  344.7 5.5 fusion.43
  350.1 0.8 compare_select_fusion.4
  350.9 0.8 gather_fusion.1
  351.8 1.2 convolution_add_fusion.2
  354.4 0.9 fusion.42
  355.3 0.9 constant_dynamic-slice_fusion.5
  356.2 68.7 %gather_fusion = bf16[16384,256]{1,0:T(8,128)(2,1)} fusion(bf16[32768,256]{1,0:T(8,128)(2,1)} %get-tuple-element.593, s32[16384]{0:T(1024)S(1)} %broadcast_clamp_fusion.2), kind=kCustom, calls=%fused_computation.1.clone.clone.1 | custom fusion | bytes 16842752 | tf_op jit(solution)/shard_map/while/body/eval_jaxpr/gather | solution.py:34
  424.9 5.5 fusion.43
  431.1 0.8 gather_fusion.1
  432.0 1.2 convolution_add_fusion.2
  434.6 0.9 fusion.42
  435.5 0.9 constant_dynamic-slice_fusion.5
  436.4 68.7 %gather_fusion = bf16[16384,256]{1,0:T(8,128)(2,1)} fusion(bf16[32768,256]{1,0:T(8,128)(2,1)} %get-tuple-element.593, s32[16384]{0:T(1024)S(1)} %broadcast_clamp_fusion.2), kind=kCustom, calls=%fused_computation.1.clone.clone.1 | custom fusion | bytes 16842752 | tf_op jit(solution)/shard_map/while/body/eval_jaxpr/gather | solution.py:34
  505.1 5.5 fusion.43
  511.4 0.8 gather_fusion.1
  512.2 1.2 convolution_add_fusion.2
  513.6 1.3 copy.45
  515.0 15.2 %fusion.11 = f32[256,256]{0,1:T(8,128)S(1)} fusion(bf16[32768,256]{0,1:T(8,128)(2,1)} %all-gather.5.cloned.1.call-done, f32[256,256]{0,1:T(8,128)} %all-reduce.3.cloned.1.call-done), kind=kOutput, calls=%fused_computation.25 | convolution fusion | flops 4295163904 | bytes 17301504 | tf_op jit(solution)/shard_map/dot_general | solution.py:28
  530.3 11.7 %cholesky.50 = f32[128,128]{1,0:T(8,128)S(1)} custom-call(f32[128,128]{1,0:T(8,128)S(1)} %cholesky.118), custom_call_target="Cholesky" | custom-call | tf_op jit(solution)/shard_map/jit(cholesky)/cholesky | solution.py:94
  542.1 9.8 %custom-call.18 = f32[1,128,128]{1,2,0:T(8,128)S(1)} custom-call(f32[1,128,128]{2,1,0:T(8,128)S(1)} %get-tuple-element.439), custom_call_target="InvertDiagBlocksLowerTriangular" | custom-call | tf_op jit(solution)/shard_map/jit(cholesky)/cholesky | solution.py:94
  552.4 11.9 %cholesky.105 = f32[128,128]{1,0:T(8,128)S(1)} custom-call(f32[128,128]{1,0:T(8,128)S(1)} %convolution_subtract_fusion.2), custom_call_target="Cholesky" | custom-call | tf_op jit(solution)/shard_map/jit(cholesky)/cholesky | solution.py:94
  566.5 4.1 while.17
  567.1 1.3 bitcast_dynamic-update-slice_fusion.2
  569.2 1.3 bitcast_dynamic-update-slice_fusion.2
  570.5 19.7 %custom-call.19 = f32[2,128,128]{1,2,0:T(8,128)S(1)} custom-call(f32[2,128,128]{2,1,0:T(8,128)S(1)} %get-tuple-element.332), custom_call_target="InvertDiagBlocksLowerTriangular" | custom-call | tf_op jit(solution)/shard_map/jit(_cho_solve)/triangular_solve | solution.py:95
  590.2 1.1 fusion.13
  591.4 1.0 convolution_subtract_fusion.1
  593.5 10.6 %all_to_all.31 = f32[128,16,16]{0,2,1:T(8,128)S(1)} all-to-all(f32[128,16,16]{0,2,1:T(8,128)S(1)} %bitcast.75), channel_id=1, replica_groups=mesh['rows'=16,'cols'=8] {'rows'}, dimensions={1} | all-to-all | bytes 262144 | tf_op jit(solution)/shard_map/all_to_all | solution.py:97
  604.2 11.2 %all_to_all.32 = f32[8,256,16]{1,2,0:T(8,128)S(1)} all-to-all(f32[8,256,16]{1,2,0:T(8,128)S(1)} %copy.47), channel_id=1, replica_groups=mesh['rows'=16,'cols'=8] {'cols'}, dimensions={0} | all-to-all | bytes 262144 | tf_op jit(solution)/shard_map/all_to_all | solution.py:96
  (61 shorter events, 13.3 us)
Async XLA Ops:
  6.5 52.8 %all-gather.3.cloned.1.call-start = ((), (), s32[]{:S(2)}) async-start(), calls=%async_computation.4 | async-start | bytes 1114112 | tf_op jit(solution)/shard_map/all_gather | solution.py:58
  7.3 162.9 %all-gather.5.cloned.1.call-start = ((), (), s32[]{:S(2)}) async-start(), calls=%async_computation.6 | async-start | bytes 17825792 | tf_op jit(solution)/shard_map/all_gather | solution.py:60
  30.5 484.4 %all-reduce.3.cloned.1.call-start = ((), (), s32[]{:S(2)}) async-start(), calls=%async_computation.5 | async-start | bytes 524288 | tf_op jit(solution)/shard_map/psum | solution.py:63
  62.1 528.1 %reduce-scatter.2.cloned.1.call-start = ((), (), s32[]{:S(2)}) async-start(), calls=%async_computation.7 | async-start | bytes 1179648 | tf_op jit(solution)/shard_map/reduce_scatter | solution.py:93
Sparse Core Ops, SparseCore 0:
  9.8 49.4 all-gather.2
  61.7 108.3 all-gather.4
  172.6 71.8 all-reduce.2
  515.1 37.6 reduce-scatter.1
where the time goes:
time: 625 us; the launch traced here: 623 us
  local copies, waits for them, and re-layouts  317 us (51%)
  waiting for transfers between devices  136 us (22%)
  other arithmetic  85.4 us (14%)
  blocking collectives  42.9 us (7%)
  matrix products  26.3 us (4%)
  between operations  14.6 us (2%)
    gather x4, local copies, waits for them, and re-layouts, block_fold(): picked = table[third.reshape(group * width)]  275 us
    all_gather x1, waiting for transfers between devices, per_device(): third_whole = lax.all_gather(third_part, 'rows', axis=1, tiled=True)  107 us
    another operation x6, other arithmetic, per_device(): factor = jnp.linalg.cholesky(gram)  34.2 us
    all_gather x1, waiting for transfers between devices, per_device(): second_range = lax.all_gather(second_factor, 'rows', axis=1, tiled=True)  28.7 us
    unnamed x3, local copies, waits for them, and re-layouts  24.6 us
    reduce_sum x4, other arithmetic, block_fold(): return jnp.sum(scaled.reshape(group, width, picked.shape[1]), axis=1)  21.8 us
    all_to_all x1, blocking collectives, from_everyone(): lax.all_to_all(jnp.broadcast_to(value[None], (size, *value.shape)), axis,...  21.1 us
    another operation x4, other arithmetic, per_device(): solved = jax.scipy.linalg.cho_solve((factor, True), mine.T).T  19.7 us
  transfers between devices with their start and end apart: 4, of which 2 were waited for; matrix products, arithmetic and copies ran while one was open for 68% of the time, Pallas kernels for 0%

commit v1 on v0

--- a/solution.py
+++ b/solution.py
@@ -57,7 +57,10 @@
     owned = jnp.arange(slab, dtype=jnp.int32)
     second_range = lax.all_gather(second_factor, "rows", axis=1, tiled=True)
     third_part = collect(third_factor, "cols", 0)
-    third_whole = lax.all_gather(third_part, "rows", axis=1, tiled=True)
+    devices = lax.axis_size("rows")
+    pieces = jnp.stack([third_part for _ in range(devices)])
+    pieces = lax.all_to_all(pieces, "rows", split_axis=0, concat_axis=0)
+    third_whole = jnp.concatenate(pieces, axis=1)
     range_rows = second_range.shape[0]
     local_gram = gram_product(second_range, second_range)
     gram_second = lax.psum(local_gram, "cols") / (range_rows * n_cols)

time: 625 us -> 725 us (1.16)
  waiting for transfers between devices: 136 us -> 223 us
  starting transfers between devices: 0.12 us -> 7.59 us
    all_gather x1, waiting for transfers between devices: 28.7 us -> 171 us  [per_device(): second_range = lax.all_gather(second_factor, 'rows', axis=1, tiled=True)]
    all_gather x1 -> x0, waiting for transfers between devices: 107 us -> none  [per_device(): third_whole = lax.all_gather(third_part, 'rows', axis=1, tiled=True)]
    all_to_all x0 -> x1, waiting for transfers between devices: none -> 50.5 us  [per_device(): pieces = lax.all_to_all(pieces, 'rows', split_axis=0, concat_axis=0)]
    all_to_all x0 -> x1, starting transfers between devices: none -> 7.47 us  [per_device(): pieces = lax.all_to_all(pieces, 'rows', split_axis=0, concat_axis=0)]
  transfers between devices with their start and end apart: 4 -> 4, of which waited for: 2 -> 2; matrix products, arithmetic and copies ran while one was open for 68% -> 58% of each run, Pallas kernels for 0% -> 0%
where the time goes in v1:
time: 725 us; the launch traced here: 723 us
  local copies, waits for them, and re-layouts  322 us (44%)
  waiting for transfers between devices  223 us (31%)
  other arithmetic  85.4 us (12%)
  blocking collectives  44.3 us (6%)
  matrix products  26.2 us (4%)
  between operations  14.6 us (2%)
  starting transfers between devices  7.59 us (1%)
    gather x4, local copies, waits for them, and re-layouts, block_fold(): picked = table[third.reshape(group * width)]  275 us
    all_gather x1, waiting for transfers between devices, per_device(): second_range = lax.all_gather(second_factor, 'rows', axis=1, tiled=True)  171 us
    all_to_all x1, waiting for transfers between devices, per_device(): pieces = lax.all_to_all(pieces, 'rows', split_axis=0, concat_axis=0)  50.5 us
    another operation x6, other arithmetic, per_device(): factor = jnp.linalg.cholesky(gram)  34.2 us
    unnamed x3, local copies, waits for them, and re-layouts  24.6 us
    reduce_sum x4, other arithmetic, block_fold(): return jnp.sum(scaled.reshape(group, width, picked.shape[1]), axis=1)  21.8 us
    all_to_all x1, blocking collectives, from_everyone(): lax.all_to_all(jnp.broadcast_to(value[None], (size, *value.shape)), axis,...  21.1 us
    another operation x4, other arithmetic, per_device(): solved = jax.scipy.linalg.cho_solve((factor, True), mine.T).T  19.7 us
  transfers between devices with their start and end apart: 4, of which 2 were waited for; matrix products, arithmetic and copies ran while one was open for 58% of the time, Pallas kernels for 0%

profile of v1, /device:TPU:0, one launch (start us, length us, event | category | flops | bytes accessed | tf_op | source)
XLA Modules:
  0.0 723.1 jit_solution(1200105981704761342)
XLA Ops:
  6.5 1.0 broadcast_in_dim.48
  7.5 21.1 %all_to_all.35 = bf16[8,4096,16]{1,2,0:T(8,128)(2,1)S(1)} all-to-all(bf16[8,4096,16]{1,2,0:T(8,128)(2,1)S(1)} %broadcast_in_dim.48), channel_id=1, replica_groups=mesh['rows'=16,'cols'=8] {'cols'}, dimensions={0} | all-to-all | bytes 2097152 | tf_op jit(solution)/shard_map/all_to_all | solution.py:17
  28.7 5.9 stack.3
  34.6 7.5 %all-to-all-start.1 = ((bf16[16,32768,16]{1,2,0:T(8,128)(2,1)}), bf16[16,32768,16]{1,2,0:T(8,128)(2,1)}, u32[]{:S(2)}, u32[]{:S(2)}) async-start(bf16[16,32768,16]{1,2,0:T(8,128)(2,1)} %stack.3), calls=%async_computation.1 | async-start | bytes 33554432 | tf_op jit(solution)/shard_map/all_to_all | solution.py:62
  42.9 171.3 %all-gather.2.cloned.1.call-done = bf16[2048,256]{0,1:T(8,128)(2,1)} async-done(((bf16[2048,16]{0,1:T(8,128)(2,1)}), bf16[2048,256]{0,1:T(8,128)(2,1)}) %all-gather.2.cloned.1.call-update) | async-done | bytes 1048592 | tf_op jit(solution)/shard_map/all_gather | solution.py:58
  214.2 2.7 fusion.24
  217.0 1.5 copy.43
  218.5 50.5 %all-to-all-done.1 = bf16[16,32768,16]{1,2,0:T(8,128)(2,1)} async-done(((bf16[16,32768,16]{1,2,0:T(8,128)(2,1)}), bf16[16,32768,16]{1,2,0:T(8,128)(2,1)}, u32[]{:S(2)}, u32[]{:S(2)}) %all-to-all-start.1) | async-done | bytes 16777248 | tf_op jit(solution)/shard_map/all_to_all | solution.py:62
  269.0 22.4 %copy.44 = bf16[32768,256]{1,0:T(8,128)(2,1)} copy(bf16[32768,256]{0,1:T(8,128)(2,1)} %bitcast.1) | data formatting | bytes 33554432
  291.4 321.0 %while.18 = (s32[]{:T(128)}, f32[1024,256]{1,0:T(8,128)S(1)}, s32[512]{0:T(512)}, s32[]{:T(128)}, s32[512]{0:T(512)}, /*index=5*/s32[]{:T(128)}, bf16[2048,256]{...) while((s32[]{:T(128)}, f32[1024,256]{1,0:T(8,128)S(1)}, ...), condition=%wide.region_7.8_spmd.clone, body=%wide.region_5.7_spmd.clone.sunk | while | flops 416057216 | bytes 28354028 | solution.py:95
  292.8 0.9 fusion.42
  293.7 0.9 constant_dynamic-slice_fusion.5
  294.6 68.7 %gather_fusion = bf16[16384,256]{1,0:T(8,128)(2,1)} fusion(bf16[32768,256]{1,0:T(8,128)(2,1)} %get-tuple-element.617, s32[16384]{0:T(1024)S(1)} %broadcast_clamp_fusion.2), kind=kCustom, calls=%fused_computation.1.clone.clone.1 | custom fusion | bytes 16842752 | tf_op jit(solution)/shard_map/while/body/eval_jaxpr/gather | solution.py:34
  363.3 5.5 fusion.43
  368.8 0.8 compare_select_fusion.4
  369.6 0.8 gather_fusion.1
  370.4 1.2 convolution_add_fusion.2
  373.1 0.9 fusion.42
  373.9 0.9 constant_dynamic-slice_fusion.5
  374.9 68.7 %gather_fusion = bf16[16384,256]{1,0:T(8,128)(2,1)} fusion(bf16[32768,256]{1,0:T(8,128)(2,1)} %get-tuple-element.617, s32[16384]{0:T(1024)S(1)} %broadcast_clamp_fusion.2), kind=kCustom, calls=%fused_computation.1.clone.clone.1 | custom fusion | bytes 16842752 | tf_op jit(solution)/shard_map/while/body/eval_jaxpr/gather | solution.py:34
  443.5 5.5 fusion.43
  449.8 0.8 gather_fusion.1
  450.6 1.2 convolution_add_fusion.2
  453.3 0.9 fusion.42
  454.1 0.9 constant_dynamic-slice_fusion.5
  455.1 68.7 %gather_fusion = bf16[16384,256]{1,0:T(8,128)(2,1)} fusion(bf16[32768,256]{1,0:T(8,128)(2,1)} %get-tuple-element.617, s32[16384]{0:T(1024)S(1)} %broadcast_clamp_fusion.2), kind=kCustom, calls=%fused_computation.1.clone.clone.1 | custom fusion | bytes 16842752 | tf_op jit(solution)/shard_map/while/body/eval_jaxpr/gather | solution.py:34
  523.7 5.5 fusion.43
  530.0 0.8 gather_fusion.1
  530.8 1.2 convolution_add_fusion.2
  533.5 0.9 fusion.42
  534.3 0.9 constant_dynamic-slice_fusion.5
  535.3 68.7 %gather_fusion = bf16[16384,256]{1,0:T(8,128)(2,1)} fusion(bf16[32768,256]{1,0:T(8,128)(2,1)} %get-tuple-element.617, s32[16384]{0:T(1024)S(1)} %broadcast_clamp_fusion.2), kind=kCustom, calls=%fused_computation.1.clone.clone.1 | custom fusion | bytes 16842752 | tf_op jit(solution)/shard_map/while/body/eval_jaxpr/gather | solution.py:34
  603.9 5.5 fusion.43
  610.2 0.8 gather_fusion.1
  611.1 1.2 convolution_add_fusion.2
  612.4 1.3 copy.45
  613.8 15.2 %fusion.11 = f32[256,256]{0,1:T(8,128)S(1)} fusion(bf16[32768,256]{0,1:T(8,128)(2,1)} %bitcast.1, f32[256,256]{0,1:T(8,128)} %all-reduce.3.cloned.1.call-done), kind=kOutput, calls=%fused_computation.25 | convolution fusion | flops 4295163904 | bytes 17301504 | tf_op jit(solution)/shard_map/dot_general | solution.py:28
  629.2 11.7 %cholesky.50 = f32[128,128]{1,0:T(8,128)S(1)} custom-call(f32[128,128]{1,0:T(8,128)S(1)} %cholesky.118), custom_call_target="Cholesky" | custom-call | tf_op jit(solution)/shard_map/jit(cholesky)/cholesky | solution.py:97
  640.9 9.8 %custom-call.18 = f32[1,128,128]{1,2,0:T(8,128)S(1)} custom-call(f32[1,128,128]{2,1,0:T(8,128)S(1)} %get-tuple-element.463), custom_call_target="InvertDiagBlocksLowerTriangular" | custom-call | tf_op jit(solution)/shard_map/jit(cholesky)/cholesky | solution.py:97
  651.3 11.9 %cholesky.105 = f32[128,128]{1,0:T(8,128)S(1)} custom-call(f32[128,128]{1,0:T(8,128)S(1)} %convolution_subtract_fusion.2), custom_call_target="Cholesky" | custom-call | tf_op jit(solution)/shard_map/jit(cholesky)/cholesky | solution.py:97
  665.3 4.1 while.17
  666.0 1.3 bitcast_dynamic-update-slice_fusion.2
  668.0 1.3 bitcast_dynamic-update-slice_fusion.2
  669.4 19.7 %custom-call.19 = f32[2,128,128]{1,2,0:T(8,128)S(1)} custom-call(f32[2,128,128]{2,1,0:T(8,128)S(1)} %get-tuple-element.332), custom_call_target="InvertDiagBlocksLowerTriangular" | custom-call | tf_op jit(solution)/shard_map/jit(_cho_solve)/triangular_solve | solution.py:98
  689.1 1.1 fusion.13
  690.2 1.0 convolution_subtract_fusion.1
  692.3 14.1 %all_to_all.36 = f32[128,16,16]{0,2,1:T(8,128)S(1)} all-to-all(f32[128,16,16]{0,2,1:T(8,128)S(1)} %bitcast.78), channel_id=1, replica_groups=mesh['rows'=16,'cols'=8] {'rows'}, dimensions={1} | all-to-all | bytes 262144 | tf_op jit(solution)/shard_map/all_to_all | solution.py:100
  706.5 9.2 %all_to_all.37 = f32[8,256,16]{1,2,0:T(8,128)S(1)} all-to-all(f32[8,256,16]{1,2,0:T(8,128)S(1)} %copy.47), channel_id=1, replica_groups=mesh['rows'=16,'cols'=8] {'cols'}, dimensions={0} | all-to-all | bytes 262144 | tf_op jit(solution)/shard_map/all_to_all | solution.py:99
  (61 shorter events, 14.1 us)
Async XLA Ops:
  34.6 234.4 %all-to-all-start.1 = ((bf16[16,32768,16]{1,2,0:T(8,128)(2,1)}), bf16[16,32768,16]{1,2,0:T(8,128)(2,1)}, u32[]{:S(2)}, u32[]{:S(2)}) async-start(bf16[16,32768,16]{1,2,0:T(8,128)(2,1)} %stack.3), calls=%async_computation.1 | async-start | bytes 33554432 | tf_op jit(solution)/shard_map/all_to_all | solution.py:62
  42.1 172.1 %all-gather.2.cloned.1.call-start = ((), (), s32[]{:S(2)}) async-start(), calls=%async_computation.5 | async-start | bytes 1114112 | tf_op jit(solution)/shard_map/all_gather | solution.py:58
  42.9 571.0 %all-reduce.3.cloned.1.call-start = ((), (), s32[]{:S(2)}) async-start(), calls=%async_computation.6 | async-start | bytes 524288 | tf_op jit(solution)/shard_map/psum | solution.py:66
  217.0 472.1 %reduce-scatter.2.cloned.1.call-start = ((), (), s32[]{:S(2)}) async-start(), calls=%async_computation.7 | async-start | bytes 1179648 | tf_op jit(solution)/shard_map/reduce_scatter | solution.py:96
Sparse Core Ops, SparseCore 0:
  45.4 168.8 all-gather.1
  217.1 91.8 all-reduce.2
  613.9 39.4 reduce-scatter.1
